TPU v7x, 256 devices: a 8x8x2 block of a 8x8x16 slice. The times are simulated.
256 devices in a mesh: parts: 2 (over z), uly: 8 (over x), blk: 16 (over y, core).
Axes of the slice: x: 8, y: 8, z: 2, core: 2. Of those that a mesh axis runs over, the one named last changes fastest.
The devices are a block of a 8x8x16 slice.
Arguments:
- queries: bfloat16 [32, 512, 8192], P(('parts', 'blk'), 'uly'), parts along dimension 0, may hold values from -4.5 to 4.5
- keys: bfloat16 [32, 512, 1024], P(('parts', 'blk'), 'uly'), parts along dimension 0, may hold values from -4.5 to 4.5
- values: bfloat16 [32, 512, 1024], P(('parts', 'blk'), 'uly'), parts along dimension 0, may hold values from -6 to 6
- doc_blocks: int32 [32], P('parts'), parts along dimension 0, may hold values from 1 to 36, 64 in all
Outputs:
- attended: bfloat16 [32, 512, 8192], P(('parts', 'blk'), 'uly'), parts along dimension 0
There are 2 independent parts, one for each index of `parts`. A program takes and returns all parts, laid end to end along the dimension named above; each array names one. Nothing has to cross between parts.
Inputs may be any that keep to these rules, and one draw needn't show every extreme that they name: `doc_blocks`: the lengths sum to 64; the longest document holds exactly (9) * 512 tokens.
All inputs are finite; a program needn't handle non-finite values.
Results may differ from a plain program's by a relative error of at most 0.0037.
Values may be sent and summed in bfloat16 or wider, within the bound.
No kernel may reach another device: no remote copies, remote signals or barrier semaphores. Data moves between devices by JAX's collectives and lax.ppermute only.
A program may use at most 128 MiB of HBM per device.

v0:
```python
import jax
import jax.numpy as jnp
from jax import lax
from jax.sharding import PartitionSpec as P

HEAD_WIDTH = 128
BLOCK = 128


def side_by_side(arrays, axis, split_dim, concat_dim, along):
    ends, at = ([], 0)
    for a in arrays[:-1]:
        at += a.shape[along]
        ends.append(at)
    both = jnp.concatenate(arrays, axis=along)
    return tuple(
        jnp.split(
            lax.all_to_all(both, axis, split_axis=split_dim, concat_axis=concat_dim, tiled=True),
            ends,
            axis=along,
        )
    )


def segment_of(positions, ends):
    return jnp.sum((positions[:, None] >= ends[None, :]).astype(jnp.int32), axis=1)


def on_device(queries, keys, values, doc_blocks):
    moved_q, moved_k, moved_v = (
        lax.all_to_all(queries, "uly", split_axis=2, concat_axis=1, tiled=True),
        *side_by_side((keys, values), "uly", 2, 1, 0),
    )
    slot = moved_q.shape[1]
    local_q = moved_q.shape[2] // HEAD_WIDTH
    local_kv = moved_k.shape[2] // HEAD_WIDTH
    query_group = local_q // local_kv
    scale = HEAD_WIDTH ** (-0.5)
    first_index = lax.axis_index("blk") * slot
    ends = jnp.cumsum(doc_blocks) * BLOCK
    qpos = first_index + jnp.arange(slot, dtype=jnp.int32)
    qseg = segment_of(qpos, ends)
    qheads = jnp.transpose(moved_q[0].reshape(slot, local_q, HEAD_WIDTH), (1, 0, 2))
    stacked = jnp.concatenate([moved_k, moved_v], axis=0)

    def allowed_for(kpos):
        kseg = segment_of(kpos, ends)
        return (qseg[:, None] == kseg[None, :]) & (kpos[None, :] <= qpos[:, None])

    start_state = (
        jnp.full((local_q, slot), -1e30, jnp.float32),
        jnp.zeros((local_q, slot), jnp.float32),
        jnp.zeros((local_q, slot, HEAD_WIDTH), jnp.float32),
    )
    piece = lax.all_gather(stacked, "blk", axis=1, tiled=True)
    start = jnp.int32(0)
    count = piece.shape[1]

    def work(state):
        key_piece = piece[0].reshape(count, local_kv, HEAD_WIDTH)
        value_piece = piece[1].reshape(count, local_kv, HEAD_WIDTH)
        allowed = allowed_for(jnp.arange(count, dtype=jnp.int32))

        def one_head(inputs):
            head, running, summed, accum = inputs
            qh = lax.dynamic_index_in_dim(qheads, head, 0, keepdims=False)
            kh = lax.dynamic_index_in_dim(key_piece, head // query_group, 1, keepdims=False)
            vh = lax.dynamic_index_in_dim(value_piece, head // query_group, 1, keepdims=False)
            scores = jnp.dot(qh, kh.T, preferred_element_type=jnp.float32) * scale
            scores = jnp.where(allowed, scores, -1e30)
            newest = jnp.maximum(running, jnp.max(scores, axis=1))
            expo = jnp.where(allowed, jnp.exp(scores - newest[:, None]), 0.0)
            factor = jnp.exp(running - newest)
            summed = summed * factor + jnp.sum(expo, axis=1)
            accum = accum * factor[:, None] + jnp.dot(
                expo.astype(jnp.bfloat16), vh, preferred_element_type=jnp.float32
            )
            return (newest, summed, accum)

        return lax.map(one_head, (jnp.arange(local_q, dtype=jnp.int32),) + tuple(state))

    last_seg = jnp.sum((start + count - 1 >= ends).astype(jnp.int32))
    useful = (start < first_index + slot) & (last_seg >= qseg[0])
    running, summed, accum = lax.cond(useful, work, lambda state: state, start_state)
    heads = (accum / summed[:, :, None]).astype(jnp.bfloat16)
    outputs = jnp.transpose(heads, (1, 0, 2)).reshape(1, slot, local_q * HEAD_WIDTH)
    return lax.all_to_all(outputs, "uly", split_axis=1, concat_axis=2, tiled=True)


def solution(mesh):
    return jax.shard_map(
        on_device,
        mesh=mesh,
        in_specs=(
            P(("parts", "blk"), "uly", None),
            P(("parts", "blk"), "uly", None),
            P(("parts", "blk"), "uly", None),
            P("parts"),
        ),
        out_specs=P(("parts", "blk"), "uly", None),
        check_vma=False,
    )
```

profile of v0, /device:TPU:720, one launch (start us, length us, event | category | flops | bytes accessed | tf_op | source)
XLA Modules:
  0.0 406.6 jit_solution(11912159211561026626)
XLA Ops:
  6.6 1.0 pad_maximum_fusion
  8.3 19.1 %all_to_all.48 = bf16[8,2,8192]{2,1,0:T(2,128)(2,1)S(1)} all-to-all(bf16[8,2,8192]{2,1,0:T(2,128)(2,1)S(1)} %reshape.78), channel_id=1, replica_groups=mesh['parts'=2,'uly'=8,'blk'=16] {'uly'}, dimensions={0} | all-to-all | bytes 524288 | tf_op jit(solution)/shard_map/all_to_all | solution.py:18
  27.8 0.9 fusion.29
  29.4 0.7 pad_maximum_fusion.1
  30.2 9.2 %copy.58 = bf16[1,64,8192]{1,0,2:T(2,128)(2,1)} copy(bf16[1,64,8192]{2,1,0:T(8,128)(2,1)} %param.8) | data formatting | bytes 2097152 | tf_op args[0]
  39.9 45.1 %reduce.2 = bf16[8192,64]{1,0:T(8,128)(2,1)S(1)} reduce(bf16[8192,1,64]{2,1,0:T(2,128)(2,1)} %bitcast.72, bf16[]{:T(256)} %broadcast.102), dimensions={1}, to_apply=%bitcast.51.reduce_sub_computation | reduce | bytes 2097154
  85.0 2.7 reshape.80
  87.6 3.8 all-to-all-start.1
  92.3 0.7 fusion.28
  94.2 24.5 %all-to-all-done.1 = bf16[8,2,32768]{2,1,0:T(2,128)(2,1)S(1)} async-done(((bf16[8,2,32768]{2,1,0:T(2,128)(2,1)}), bf16[8,2,32768]{2,1,0:T(2,128)(2,1)S(1)}, u32[]{:S(2)}, u32[]{:S(2)}) %all-to-all-start.1) | async-done | bytes 1048608 | tf_op jit(solution)/shard_map/all_to_all | solution.py:31
  118.7 4.3 %reshape.81 = bf16[8192,1,64]{2,1,0:T(2,128)(2,1)} reshape(bf16[8,2,32768]{2,1,0:T(2,128)(2,1)S(1)} %all-to-all-done.1) | data formatting | bytes 2097152
  123.1 8.2 %copy.59 = bf16[1,64,8192]{2,1,0:T(8,128)(2,1)S(1)} copy(bf16[1,64,8192]{1,0,2:T(2,128)(2,1)} %bitcast.73) | data formatting | bytes 2097152 | tf_op jit(solution)/shard_map/all_to_all | solution.py:31
  132.8 221.4 %conditional.1 = (f32[8,512]{1,0:T(8,128)}, f32[8,512,128]{1,2,0:T(8,128)}) conditional(s32[]{:T(128)} %convert_element_type.20, () %tuple.17, (bf16[2,8192,128]{2,1,0:T(8,128)(2,1)}, s32[512]{0:T(512)S(1)}, s32[16]{0:T(128)S(1)}, s32[]{:T(128)}, s32[512]{0:T(512)S(1)}, /*index=5*/bf16[8,512,128]{2,0,1:T(8,128)(2,1)S(1)}) %tuple.53), branch_computations={%region_3.4_spmd, %region_4.10_spmd} | conditional | flops 2240210944 | bytes 133736896 | solution.py:84
  133.0 1.1 copy.61
  134.2 3.8 slice_bitcast_fusion
  138.2 216.0 %while.12 = (s32[]{:T(128)}, f32[8,512]{1,0:T(8,128)}, f32[8,512,128]{1,2,0:T(8,128)}, s32[8]{0:T(128)S(1)}, bf16[8,512,128]{2,1,0:T(8,128)(2,1)}, /*index=5*/bf...) while((s32[]{:T(128)}, f32[8,512]{1,0:T(8,128)}, ...), condition=%wide.region_9.9_spmd.clone, body=%wide.region_6.8_spmd.clone.sunk | while | flops 2239825408 | bytes 123214048 | solution.py:80
  138.2 0.7 dynamic_slice.27
  141.0 6.8 %fusion.37 = (f32[512]{0:T(512)S(1)}, f32[512,8192]{1,0:T(8,128)S(1)}) fusion(s32[512]{0:T(512)S(1)} %get-tuple-element.266, s32[8192]{0:T(1024)S(1)} %get-tuple-element.264, s32[512]{0:T(512)S(1)} %get-tuple-element.265, bf16[8192,1,128]{2,0,1:T(8,128)(2,1)} %get-tuple-element.262, bf16[8,512,128]{2,1,0:T(8,128)(2,1)} %get-tuple-element.261, ...), kind=kOutput, calls=%fused_computation.5.clone.1 | convolution fusion | flops 1098907136 | bytes 19044356 | tf_op jit(solution)/shard_map/cond/branch_1_fun/while/body/eval_jaxpr/dot_general | solution.py:69
  147.8 6.2 %fusion.38 = f32[512]{0:T(512)S(1)} fusion(f32[512,8192]{1,0:T(8,128)S(1)} %get-tuple-element.228, s32[512]{0:T(512)S(1)} %get-tuple-element.266, s32[8192]{0:T(1024)S(1)} %get-tuple-element.264, f32[512]{0:T(512)S(1)} %broadcast_maximum_fusion.2, s32[512]{0:T(512)S(1)} %get-tuple-element.265), kind=kLoop, calls=%fused_computation.7.clone.1 | loop fusion | flops 33553920 | bytes 16818176 | tf_op jit(solution)/shard_map/cond/branch_1_fun/while/body/eval_jaxpr/reduce_sum | solution.py:74
  153.9 1.3 dynamic_update_slice.14
  155.3 9.1 %fusion.39 = f32[1,512,128]{2,1,0:T(8,128)S(1)} fusion(bf16[8192,1,128]{2,0,1:T(8,128)(2,1)S(1)} %get-tuple-element.263, f32[512,8192]{1,0:T(8,128)} %copy-done, s32[512]{0:T(512)S(1)} %get-tuple-element.266, s32[8192]{0:T(1024)S(1)} %get-tuple-element.264, f32[512]{0:T(512)S(1)} %broadcast_maximum_fusion.2, s32[512]{0:T(512)S(1)} %get-tuple-element.265, ...), kind=kOutput, calls=%fused_computation.13.clone.1 | convolution fusion | flops 1107361792 | bytes 19177472 | tf_op jit(solution)/shard_map/cond/branch_1_fun/while/body/eval_jaxpr/dot_general | solution.py:75
  164.5 0.7 constant_dynamic-update-slice_fusion.2
  168.0 6.8 %fusion.37 = (f32[512]{0:T(512)S(1)}, f32[512,8192]{1,0:T(8,128)S(1)}) fusion(s32[512]{0:T(512)S(1)} %get-tuple-element.266, s32[8192]{0:T(1024)S(1)} %get-tuple-element.264, s32[512]{0:T(512)S(1)} %get-tuple-element.265, bf16[8192,1,128]{2,0,1:T(8,128)(2,1)} %get-tuple-element.262, bf16[8,512,128]{2,1,0:T(8,128)(2,1)} %get-tuple-element.261, ...), kind=kOutput, calls=%fused_computation.5.clone.1 | convolution fusion | flops 1098907136 | bytes 19044356 | tf_op jit(solution)/shard_map/cond/branch_1_fun/while/body/eval_jaxpr/dot_general | solution.py:69
  174.8 6.2 %fusion.38 = f32[512]{0:T(512)S(1)} fusion(f32[512,8192]{1,0:T(8,128)S(1)} %get-tuple-element.228, s32[512]{0:T(512)S(1)} %get-tuple-element.266, s32[8192]{0:T(1024)S(1)} %get-tuple-element.264, f32[512]{0:T(512)S(1)} %broadcast_maximum_fusion.2, s32[512]{0:T(512)S(1)} %get-tuple-element.265), kind=kLoop, calls=%fused_computation.7.clone.1 | loop fusion | flops 33553920 | bytes 16818176 | tf_op jit(solution)/shard_map/cond/branch_1_fun/while/body/eval_jaxpr/reduce_sum | solution.py:74
  180.9 1.3 dynamic_update_slice.14
  182.3 9.1 %fusion.39 = f32[1,512,128]{2,1,0:T(8,128)S(1)} fusion(bf16[8192,1,128]{2,0,1:T(8,128)(2,1)S(1)} %get-tuple-element.263, f32[512,8192]{1,0:T(8,128)} %copy-done, s32[512]{0:T(512)S(1)} %get-tuple-element.266, s32[8192]{0:T(1024)S(1)} %get-tuple-element.264, f32[512]{0:T(512)S(1)} %broadcast_maximum_fusion.2, s32[512]{0:T(512)S(1)} %get-tuple-element.265, ...), kind=kOutput, calls=%fused_computation.13.clone.1 | convolution fusion | flops 1107361792 | bytes 19177472 | tf_op jit(solution)/shard_map/cond/branch_1_fun/while/body/eval_jaxpr/dot_general | solution.py:75
  191.5 0.7 constant_dynamic-update-slice_fusion.2
  194.9 6.8 %fusion.37 = (f32[512]{0:T(512)S(1)}, f32[512,8192]{1,0:T(8,128)S(1)}) fusion(s32[512]{0:T(512)S(1)} %get-tuple-element.266, s32[8192]{0:T(1024)S(1)} %get-tuple-element.264, s32[512]{0:T(512)S(1)} %get-tuple-element.265, bf16[8192,1,128]{2,0,1:T(8,128)(2,1)} %get-tuple-element.262, bf16[8,512,128]{2,1,0:T(8,128)(2,1)} %get-tuple-element.261, ...), kind=kOutput, calls=%fused_computation.5.clone.1 | convolution fusion | flops 1098907136 | bytes 19044356 | tf_op jit(solution)/shard_map/cond/branch_1_fun/while/body/eval_jaxpr/dot_general | solution.py:69
  201.8 6.2 %fusion.38 = f32[512]{0:T(512)S(1)} fusion(f32[512,8192]{1,0:T(8,128)S(1)} %get-tuple-element.228, s32[512]{0:T(512)S(1)} %get-tuple-element.266, s32[8192]{0:T(1024)S(1)} %get-tuple-element.264, f32[512]{0:T(512)S(1)} %broadcast_maximum_fusion.2, s32[512]{0:T(512)S(1)} %get-tuple-element.265), kind=kLoop, calls=%fused_computation.7.clone.1 | loop fusion | flops 33553920 | bytes 16818176 | tf_op jit(solution)/shard_map/cond/branch_1_fun/while/body/eval_jaxpr/reduce_sum | solution.py:74
  208.0 1.3 dynamic_update_slice.14
  209.3 9.1 %fusion.39 = f32[1,512,128]{2,1,0:T(8,128)S(1)} fusion(bf16[8192,1,128]{2,0,1:T(8,128)(2,1)S(1)} %get-tuple-element.263, f32[512,8192]{1,0:T(8,128)} %copy-done, s32[512]{0:T(512)S(1)} %get-tuple-element.266, s32[8192]{0:T(1024)S(1)} %get-tuple-element.264, f32[512]{0:T(512)S(1)} %broadcast_maximum_fusion.2, s32[512]{0:T(512)S(1)} %get-tuple-element.265, ...), kind=kOutput, calls=%fused_computation.13.clone.1 | convolution fusion | flops 1107361792 | bytes 19177472 | tf_op jit(solution)/shard_map/cond/branch_1_fun/while/body/eval_jaxpr/dot_general | solution.py:75
  218.5 0.7 constant_dynamic-update-slice_fusion.2
  222.0 6.8 %fusion.37 = (f32[512]{0:T(512)S(1)}, f32[512,8192]{1,0:T(8,128)S(1)}) fusion(s32[512]{0:T(512)S(1)} %get-tuple-element.266, s32[8192]{0:T(1024)S(1)} %get-tuple-element.264, s32[512]{0:T(512)S(1)} %get-tuple-element.265, bf16[8192,1,128]{2,0,1:T(8,128)(2,1)} %get-tuple-element.262, bf16[8,512,128]{2,1,0:T(8,128)(2,1)} %get-tuple-element.261, ...), kind=kOutput, calls=%fused_computation.5.clone.1 | convolution fusion | flops 1098907136 | bytes 19044356 | tf_op jit(solution)/shard_map/cond/branch_1_fun/while/body/eval_jaxpr/dot_general | solution.py:69
  228.8 6.2 %fusion.38 = f32[512]{0:T(512)S(1)} fusion(f32[512,8192]{1,0:T(8,128)S(1)} %get-tuple-element.228, s32[512]{0:T(512)S(1)} %get-tuple-element.266, s32[8192]{0:T(1024)S(1)} %get-tuple-element.264, f32[512]{0:T(512)S(1)} %broadcast_maximum_fusion.2, s32[512]{0:T(512)S(1)} %get-tuple-element.265), kind=kLoop, calls=%fused_computation.7.clone.1 | loop fusion | flops 33553920 | bytes 16818176 | tf_op jit(solution)/shard_map/cond/branch_1_fun/while/body/eval_jaxpr/reduce_sum | solution.py:74
  235.0 1.3 dynamic_update_slice.14
  236.3 9.1 %fusion.39 = f32[1,512,128]{2,1,0:T(8,128)S(1)} fusion(bf16[8192,1,128]{2,0,1:T(8,128)(2,1)S(1)} %get-tuple-element.263, f32[512,8192]{1,0:T(8,128)} %copy-done, s32[512]{0:T(512)S(1)} %get-tuple-element.266, s32[8192]{0:T(1024)S(1)} %get-tuple-element.264, f32[512]{0:T(512)S(1)} %broadcast_maximum_fusion.2, s32[512]{0:T(512)S(1)} %get-tuple-element.265, ...), kind=kOutput, calls=%fused_computation.13.clone.1 | convolution fusion | flops 1107361792 | bytes 19177472 | tf_op jit(solution)/shard_map/cond/branch_1_fun/while/body/eval_jaxpr/dot_general | solution.py:75
  245.5 0.7 constant_dynamic-update-slice_fusion.2
  249.0 6.8 %fusion.37 = (f32[512]{0:T(512)S(1)}, f32[512,8192]{1,0:T(8,128)S(1)}) fusion(s32[512]{0:T(512)S(1)} %get-tuple-element.266, s32[8192]{0:T(1024)S(1)} %get-tuple-element.264, s32[512]{0:T(512)S(1)} %get-tuple-element.265, bf16[8192,1,128]{2,0,1:T(8,128)(2,1)} %get-tuple-element.262, bf16[8,512,128]{2,1,0:T(8,128)(2,1)} %get-tuple-element.261, ...), kind=kOutput, calls=%fused_computation.5.clone.1 | convolution fusion | flops 1098907136 | bytes 19044356 | tf_op jit(solution)/shard_map/cond/branch_1_fun/while/body/eval_jaxpr/dot_general | solution.py:69
  255.8 6.2 %fusion.38 = f32[512]{0:T(512)S(1)} fusion(f32[512,8192]{1,0:T(8,128)S(1)} %get-tuple-element.228, s32[512]{0:T(512)S(1)} %get-tuple-element.266, s32[8192]{0:T(1024)S(1)} %get-tuple-element.264, f32[512]{0:T(512)S(1)} %broadcast_maximum_fusion.2, s32[512]{0:T(512)S(1)} %get-tuple-element.265), kind=kLoop, calls=%fused_computation.7.clone.1 | loop fusion | flops 33553920 | bytes 16818176 | tf_op jit(solution)/shard_map/cond/branch_1_fun/while/body/eval_jaxpr/reduce_sum | solution.py:74
  262.0 1.3 dynamic_update_slice.14
  263.3 9.1 %fusion.39 = f32[1,512,128]{2,1,0:T(8,128)S(1)} fusion(bf16[8192,1,128]{2,0,1:T(8,128)(2,1)S(1)} %get-tuple-element.263, f32[512,8192]{1,0:T(8,128)} %copy-done, s32[512]{0:T(512)S(1)} %get-tuple-element.266, s32[8192]{0:T(1024)S(1)} %get-tuple-element.264, f32[512]{0:T(512)S(1)} %broadcast_maximum_fusion.2, s32[512]{0:T(512)S(1)} %get-tuple-element.265, ...), kind=kOutput, calls=%fused_computation.13.clone.1 | convolution fusion | flops 1107361792 | bytes 19177472 | tf_op jit(solution)/shard_map/cond/branch_1_fun/while/body/eval_jaxpr/dot_general | solution.py:75
  272.5 0.7 constant_dynamic-update-slice_fusion.2
  276.0 6.8 %fusion.37 = (f32[512]{0:T(512)S(1)}, f32[512,8192]{1,0:T(8,128)S(1)}) fusion(s32[512]{0:T(512)S(1)} %get-tuple-element.266, s32[8192]{0:T(1024)S(1)} %get-tuple-element.264, s32[512]{0:T(512)S(1)} %get-tuple-element.265, bf16[8192,1,128]{2,0,1:T(8,128)(2,1)} %get-tuple-element.262, bf16[8,512,128]{2,1,0:T(8,128)(2,1)} %get-tuple-element.261, ...), kind=kOutput, calls=%fused_computation.5.clone.1 | convolution fusion | flops 1098907136 | bytes 19044356 | tf_op jit(solution)/shard_map/cond/branch_1_fun/while/body/eval_jaxpr/dot_general | solution.py:69
  282.8 6.2 %fusion.38 = f32[512]{0:T(512)S(1)} fusion(f32[512,8192]{1,0:T(8,128)S(1)} %get-tuple-element.228, s32[512]{0:T(512)S(1)} %get-tuple-element.266, s32[8192]{0:T(1024)S(1)} %get-tuple-element.264, f32[512]{0:T(512)S(1)} %broadcast_maximum_fusion.2, s32[512]{0:T(512)S(1)} %get-tuple-element.265), kind=kLoop, calls=%fused_computation.7.clone.1 | loop fusion | flops 33553920 | bytes 16818176 | tf_op jit(solution)/shard_map/cond/branch_1_fun/while/body/eval_jaxpr/reduce_sum | solution.py:74
  288.9 1.3 dynamic_update_slice.14
  290.3 9.1 %fusion.39 = f32[1,512,128]{2,1,0:T(8,128)S(1)} fusion(bf16[8192,1,128]{2,0,1:T(8,128)(2,1)S(1)} %get-tuple-element.263, f32[512,8192]{1,0:T(8,128)} %copy-done, s32[512]{0:T(512)S(1)} %get-tuple-element.266, s32[8192]{0:T(1024)S(1)} %get-tuple-element.264, f32[512]{0:T(512)S(1)} %broadcast_maximum_fusion.2, s32[512]{0:T(512)S(1)} %get-tuple-element.265, ...), kind=kOutput, calls=%fused_computation.13.clone.1 | convolution fusion | flops 1107361792 | bytes 19177472 | tf_op jit(solution)/shard_map/cond/branch_1_fun/while/body/eval_jaxpr/dot_general | solution.py:75
  299.5 0.7 constant_dynamic-update-slice_fusion.2
  302.9 6.8 %fusion.37 = (f32[512]{0:T(512)S(1)}, f32[512,8192]{1,0:T(8,128)S(1)}) fusion(s32[512]{0:T(512)S(1)} %get-tuple-element.266, s32[8192]{0:T(1024)S(1)} %get-tuple-element.264, s32[512]{0:T(512)S(1)} %get-tuple-element.265, bf16[8192,1,128]{2,0,1:T(8,128)(2,1)} %get-tuple-element.262, bf16[8,512,128]{2,1,0:T(8,128)(2,1)} %get-tuple-element.261, ...), kind=kOutput, calls=%fused_computation.5.clone.1 | convolution fusion | flops 1098907136 | bytes 19044356 | tf_op jit(solution)/shard_map/cond/branch_1_fun/while/body/eval_jaxpr/dot_general | solution.py:69
  309.8 6.2 %fusion.38 = f32[512]{0:T(512)S(1)} fusion(f32[512,8192]{1,0:T(8,128)S(1)} %get-tuple-element.228, s32[512]{0:T(512)S(1)} %get-tuple-element.266, s32[8192]{0:T(1024)S(1)} %get-tuple-element.264, f32[512]{0:T(512)S(1)} %broadcast_maximum_fusion.2, s32[512]{0:T(512)S(1)} %get-tuple-element.265), kind=kLoop, calls=%fused_computation.7.clone.1 | loop fusion | flops 33553920 | bytes 16818176 | tf_op jit(solution)/shard_map/cond/branch_1_fun/while/body/eval_jaxpr/reduce_sum | solution.py:74
  316.0 1.3 dynamic_update_slice.14
  317.3 9.1 %fusion.39 = f32[1,512,128]{2,1,0:T(8,128)S(1)} fusion(bf16[8192,1,128]{2,0,1:T(8,128)(2,1)S(1)} %get-tuple-element.263, f32[512,8192]{1,0:T(8,128)} %copy-done, s32[512]{0:T(512)S(1)} %get-tuple-element.266, s32[8192]{0:T(1024)S(1)} %get-tuple-element.264, f32[512]{0:T(512)S(1)} %broadcast_maximum_fusion.2, s32[512]{0:T(512)S(1)} %get-tuple-element.265, ...), kind=kOutput, calls=%fused_computation.13.clone.1 | convolution fusion | flops 1107361792 | bytes 19177472 | tf_op jit(solution)/shard_map/cond/branch_1_fun/while/body/eval_jaxpr/dot_general | solution.py:75
  326.5 0.7 constant_dynamic-update-slice_fusion.2
  329.9 6.8 %fusion.37 = (f32[512]{0:T(512)S(1)}, f32[512,8192]{1,0:T(8,128)S(1)}) fusion(s32[512]{0:T(512)S(1)} %get-tuple-element.266, s32[8192]{0:T(1024)S(1)} %get-tuple-element.264, s32[512]{0:T(512)S(1)} %get-tuple-element.265, bf16[8192,1,128]{2,0,1:T(8,128)(2,1)} %get-tuple-element.262, bf16[8,512,128]{2,1,0:T(8,128)(2,1)} %get-tuple-element.261, ...), kind=kOutput, calls=%fused_computation.5.clone.1 | convolution fusion | flops 1098907136 | bytes 19044356 | tf_op jit(solution)/shard_map/cond/branch_1_fun/while/body/eval_jaxpr/dot_general | solution.py:69
  336.7 6.2 %fusion.38 = f32[512]{0:T(512)S(1)} fusion(f32[512,8192]{1,0:T(8,128)S(1)} %get-tuple-element.228, s32[512]{0:T(512)S(1)} %get-tuple-element.266, s32[8192]{0:T(1024)S(1)} %get-tuple-element.264, f32[512]{0:T(512)S(1)} %broadcast_maximum_fusion.2, s32[512]{0:T(512)S(1)} %get-tuple-element.265), kind=kLoop, calls=%fused_computation.7.clone.1 | loop fusion | flops 33553920 | bytes 16818176 | tf_op jit(solution)/shard_map/cond/branch_1_fun/while/body/eval_jaxpr/reduce_sum | solution.py:74
  342.9 1.3 dynamic_update_slice.14
  344.3 9.1 %fusion.39 = f32[1,512,128]{2,1,0:T(8,128)S(1)} fusion(bf16[8192,1,128]{2,0,1:T(8,128)(2,1)S(1)} %get-tuple-element.263, f32[512,8192]{1,0:T(8,128)} %copy-done, s32[512]{0:T(512)S(1)} %get-tuple-element.266, s32[8192]{0:T(1024)S(1)} %get-tuple-element.264, f32[512]{0:T(512)S(1)} %broadcast_maximum_fusion.2, s32[512]{0:T(512)S(1)} %get-tuple-element.265, ...), kind=kOutput, calls=%fused_computation.13.clone.1 | convolution fusion | flops 1107361792 | bytes 19177472 | tf_op jit(solution)/shard_map/cond/branch_1_fun/while/body/eval_jaxpr/dot_general | solution.py:75
  353.5 0.7 constant_dynamic-update-slice_fusion.2
  354.2 1.9 divide_convert_fusion
  356.1 2.0 copy.63
  358.1 6.7 %reduce.3 = bf16[512,1024]{1,0:T(8,128)(2,1)S(1)} reduce(bf16[512,1,1024]{2,1,0:T(2,128)(2,1)S(1)} %bitcast.75, bf16[]{:T(256)} %broadcast.102), dimensions={1}, to_apply=%bitcast.53.reduce_sub_computation | reduce | bytes 2097154
  364.8 0.8 reshape.82
  365.6 31.7 %all_to_all.49 = bf16[8,2,32768]{2,1,0:T(2,128)(2,1)S(1)} all-to-all(bf16[8,2,32768]{2,1,0:T(2,128)(2,1)S(1)} %reshape.82), channel_id=1, replica_groups=mesh['parts'=2,'uly'=8,'blk'=16] {'uly'}, dimensions={0} | all-to-all | bytes 2097152 | tf_op jit(solution)/shard_map/all_to_all | solution.py:87
  397.2 1.0 reshape.83
  398.7 1.1 copy.70
  (75 shorter events, 11.1 us)
Async XLA Ops:
  6.5 126.2 %all-gather.2.cloned.1.call-start = ((), (), s32[]{:S(2)}) async-start(), calls=%async_computation.3 | async-start | bytes 4456448 | tf_op jit(solution)/shard_map/all_gather | solution.py:55
  30.2 61.3 %copy-start.1 = (s32[16]{0:T(128)S(1)}, s32[16]{0:T(128)}, u32[]{:S(2)}) copy-start(s32[16]{0:T(128)} %param.11) | copy-start | bytes 196
  87.6 31.1 %all-to-all-start.1 = ((bf16[8,2,32768]{2,1,0:T(2,128)(2,1)}), bf16[8,2,32768]{2,1,0:T(2,128)(2,1)S(1)}, u32[]{:S(2)}, u32[]{:S(2)}) async-start(bf16[8,2,32768]{2,1,0:T(2,128)(2,1)} %reshape.80), calls=%async_computation.1 | async-start | bytes 2097152 | tf_op jit(solution)/shard_map/all_to_all | solution.py:31
  147.7 6.2 %copy-start = (f32[512,8192]{1,0:T(8,128)}, f32[512,8192]{1,0:T(8,128)S(1)}, u32[]{:S(2)}) copy-start(f32[512,8192]{1,0:T(8,128)S(1)} %get-tuple-element.228) | copy-start | bytes 50331652 | tf_op jit(solution)/shard_map/cond/branch_1_fun/while
  174.7 6.2 %copy-start = (f32[512,8192]{1,0:T(8,128)}, f32[512,8192]{1,0:T(8,128)S(1)}, u32[]{:S(2)}) copy-start(f32[512,8192]{1,0:T(8,128)S(1)} %get-tuple-element.228) | copy-start | bytes 50331652 | tf_op jit(solution)/shard_map/cond/branch_1_fun/while
  201.7 6.2 %copy-start = (f32[512,8192]{1,0:T(8,128)}, f32[512,8192]{1,0:T(8,128)S(1)}, u32[]{:S(2)}) copy-start(f32[512,8192]{1,0:T(8,128)S(1)} %get-tuple-element.228) | copy-start | bytes 50331652 | tf_op jit(solution)/shard_map/cond/branch_1_fun/while
  228.7 6.2 %copy-start = (f32[512,8192]{1,0:T(8,128)}, f32[512,8192]{1,0:T(8,128)S(1)}, u32[]{:S(2)}) copy-start(f32[512,8192]{1,0:T(8,128)S(1)} %get-tuple-element.228) | copy-start | bytes 50331652 | tf_op jit(solution)/shard_map/cond/branch_1_fun/while
  255.8 6.2 %copy-start = (f32[512,8192]{1,0:T(8,128)}, f32[512,8192]{1,0:T(8,128)S(1)}, u32[]{:S(2)}) copy-start(f32[512,8192]{1,0:T(8,128)S(1)} %get-tuple-element.228) | copy-start | bytes 50331652 | tf_op jit(solution)/shard_map/cond/branch_1_fun/while
  282.7 6.2 %copy-start = (f32[512,8192]{1,0:T(8,128)}, f32[512,8192]{1,0:T(8,128)S(1)}, u32[]{:S(2)}) copy-start(f32[512,8192]{1,0:T(8,128)S(1)} %get-tuple-element.228) | copy-start | bytes 50331652 | tf_op jit(solution)/shard_map/cond/branch_1_fun/while
  309.7 6.2 %copy-start = (f32[512,8192]{1,0:T(8,128)}, f32[512,8192]{1,0:T(8,128)S(1)}, u32[]{:S(2)}) copy-start(f32[512,8192]{1,0:T(8,128)S(1)} %get-tuple-element.228) | copy-start | bytes 50331652 | tf_op jit(solution)/shard_map/cond/branch_1_fun/while
  336.7 6.2 %copy-start = (f32[512,8192]{1,0:T(8,128)}, f32[512,8192]{1,0:T(8,128)S(1)}, u32[]{:S(2)}) copy-start(f32[512,8192]{1,0:T(8,128)S(1)} %get-tuple-element.228) | copy-start | bytes 50331652 | tf_op jit(solution)/shard_map/cond/branch_1_fun/while
Sparse Core Ops, SparseCore 0:
  30.3 37.7 all-gather.1
where the time goes:
time: 408 us; the launch traced here: 407 us
  matrix products  127 us (31%)
  other arithmetic  106 us (26%)
  local copies, waits for them, and re-layouts  62.7 us (15%)
  blocking collectives  50.7 us (12%)
  waiting for transfers between devices  24.6 us (6%)
  loops' own time  17.2 us (4%)
  between operations  14.8 us (4%)
    dot_general x8, matrix products, one_head(): jnp.dot(expo.astype(jnp.bfloat16), vh, preferred_element_type=jnp.float32)  72.5 us
    dot_general x8, matrix products, one_head(): scores = jnp.dot(qh, kh.T, preferred_element_type=jnp.float32) * scale  54.3 us
    unnamed x2, other arithmetic  51.8 us
    reduce_sum x8, other arithmetic, one_head(): summed = summed * factor + jnp.sum(expo, axis=1)  49.4 us
    all_to_all x1, blocking collectives, on_device(): lax.all_to_all(outputs, 'uly', split_axis=1, concat_axis=2, tiled=True)  31.7 us
    all_to_all x1, waiting for transfers between devices, on_device(): lax.all_to_all(queries, 'uly', split_axis=2, concat_axis=1, tiled=True)  24.5 us
    unnamed x13, local copies, waits for them, and re-layouts  20.5 us
    all_to_all x1, blocking collectives, side_by_side(): lax.all_to_all(both, axis, split_axis=split_dim, concat_axis=concat_dim,...  19.1 us
  transfers between devices with their start and end apart: 2, of which 1 were waited for; matrix products, arithmetic and copies ran while one was open for 18% of the time, Pallas kernels for 0%

commit v1 on v0

--- a/solution.py
+++ b/solution.py
@@ -5,6 +5,15 @@
 
 HEAD_WIDTH = 128
 BLOCK = 128
+
+
+def widths_list(mine_x):
+    carry_out = lax.axis_size("uly")
+    vec_out = jnp.split(mine_x, carry_out, 2)
+    all_values = jnp.stack(vec_out)
+    z_new = lax.all_to_all(all_values, axis_name="uly", split_axis=0, concat_axis=0)
+    mat_out = jnp.concatenate(z_new, 1)
+    return mat_out
 
 
 def side_by_side(arrays, axis, split_dim, concat_dim, along):
@@ -28,7 +37,7 @@
 
 def on_device(queries, keys, values, doc_blocks):
     moved_q, moved_k, moved_v = (
-        lax.all_to_all(queries, "uly", split_axis=2, concat_axis=1, tiled=True),
+        widths_list(queries),
         *side_by_side((keys, values), "uly", 2, 1, 0),
     )
     slot = moved_q.shape[1]

time: 408 us -> 411 us (level)
  the two profiles are of different devices: /device:TPU:720 before, /device:TPU:513 now
where the time goes in v1:
time: 411 us; the launch traced here: 410 us
  matrix products  127 us (31%)
  local copies, waits for them, and re-layouts  96 us (23%)
  other arithmetic  60.8 us (15%)
  blocking collectives  51.3 us (12%)
  waiting for transfers between devices  39.4 us (10%)
  loops' own time  16.9 us (4%)
  between operations  14.8 us (4%)
    dot_general x8, matrix products, one_head(): jnp.dot(expo.astype(jnp.bfloat16), vh, preferred_element_type=jnp.float32)  72.5 us
    dot_general x8, matrix products, one_head(): scores = jnp.dot(qh, kh.T, preferred_element_type=jnp.float32) * scale  54.2 us
    reduce_sum x8, other arithmetic, one_head(): summed = summed * factor + jnp.sum(expo, axis=1)  49.2 us
    while x16, local copies, waits for them, and re-layouts  45.6 us
    all_to_all x1, blocking collectives, on_device(): lax.all_to_all(outputs, 'uly', split_axis=1, concat_axis=2, tiled=True)  34.3 us
    all_gather x1, waiting for transfers between devices, on_device(): piece = lax.all_gather(stacked, 'blk', axis=1, tiled=True)  26.5 us
    dynamic_update_slice x24, local copies, waits for them, and re-layouts, work(): lax.map(one_head, (jnp.arange(local_q, dtype=jnp.int32),) + tuple(state))  17.5 us
    all_to_all x1, blocking collectives, side_by_side(): lax.all_to_all(both, axis, split_axis=split_dim, concat_axis=concat_dim,...  17 us
  transfers between devices with their start and end apart: 2, of which 2 were waited for; matrix products, arithmetic and copies ran while one was open for 4% of the time, Pallas kernels for 0%

profile of v1, /device:TPU:513, one launch (start us, length us, event | category | flops | bytes accessed | tf_op | source)
XLA Modules:
  0.0 409.7 jit_solution(16165551560217072339)
XLA Ops:
  6.6 1.0 pad_maximum_fusion
  8.3 17.0 %all_to_all.38 = bf16[8,2,8192]{2,1,0:T(2,128)(2,1)S(1)} all-to-all(bf16[8,2,8192]{2,1,0:T(2,128)(2,1)S(1)} %reshape.77), channel_id=1, replica_groups=mesh['parts'=2,'uly'=8,'blk'=16] {'uly'}, dimensions={0} | all-to-all | bytes 524288 | tf_op jit(solution)/shard_map/all_to_all | solution.py:27
  25.7 0.9 fusion.29
  28.1 1.6 bitcast_dynamic-update-slice_fusion.7
  29.7 1.6 bitcast_dynamic-update-slice_fusion.6
  31.2 1.6 bitcast_dynamic-update-slice_fusion.5
  32.8 1.6 bitcast_dynamic-update-slice_fusion.4
  34.4 1.6 bitcast_dynamic-update-slice_fusion.3
  35.9 1.6 bitcast_dynamic-update-slice_fusion.2
  37.5 1.6 bitcast_dynamic-update-slice_fusion.1
  39.1 1.6 bitcast_dynamic-update-slice_fusion
  40.6 3.8 all-to-all-start.1
  47.8 12.9 %all-to-all-done.1 = bf16[8,1,64,1024]{3,2,1,0:T(8,128)(2,1)S(1)} async-done(((bf16[8,1,64,1024]{3,2,1,0:T(8,128)(2,1)}), bf16[8,1,64,1024]{3,2,1,0:T(8,128)(2,1)S(1)}, u32[]{:S(2)}, u32[]{:S(2)}) %all-to-all-start.1) | async-done | bytes 1048608 | tf_op jit(solution)/shard_map/all_to_all | solution.py:14
  61.0 26.5 %all-gather.2.cloned.1.call-done = bf16[2,8192,128]{2,1,0:T(8,128)(2,1)} async-done(((bf16[2,512,128]{2,1,0:T(8,128)(2,1)}), bf16[2,8192,128]{2,1,0:T(8,128)(2,1)}) %all-gather.2.cloned.1.call-update) | async-done | bytes 4194320 | tf_op jit(solution)/shard_map/all_gather | solution.py:64
  87.5 266.6 %conditional.1 = (f32[8,512]{1,0:T(8,128)}, f32[8,512,128]{1,2,0:T(8,128)}) conditional(s32[]{:T(128)} %convert_element_type.20, () %tuple.17, (bf16[2,8192,128]{2,1,0:T(8,128)(2,1)}, s32[512]{0:T(512)S(1)}, s32[16]{0:T(128)S(1)}, s32[]{:T(128)}, s32[512]{0:T(512)S(1)}, /*index=5*/bf16[8,512,128]{2,0,1:T(8,128)(2,1)S(1)}) %tuple.52), branch_computations={%region_3.4_spmd, %region_4.10_spmd} | conditional | flops 2240210944 | bytes 133736896 | solution.py:93
  87.5 1.1 copy.39
  88.6 3.8 slice_bitcast_fusion
  92.6 261.4 %while.12 = (s32[]{:T(128)}, f32[8,512]{1,0:T(8,128)}, f32[8,512,128]{1,2,0:T(8,128)}, s32[8]{0:T(128)S(1)}, bf16[8,512,128]{2,1,0:T(8,128)(2,1)}, /*index=5*/bf...) while((s32[]{:T(128)}, f32[8,512]{1,0:T(8,128)}, ...), condition=%wide.region_9.9_spmd.clone, body=%wide.region_6.8_spmd.clone.sunk | while | flops 2239825408 | bytes 123214048 | solution.py:89
  95.4 6.8 %fusion.37 = (f32[512]{0:T(512)S(1)}, f32[512,8192]{1,0:T(8,128)S(1)}) fusion(s32[512]{0:T(512)S(1)} %get-tuple-element.260, s32[8192]{0:T(1024)S(1)} %get-tuple-element.258, s32[512]{0:T(512)S(1)} %get-tuple-element.259, bf16[8192,1,128]{2,0,1:T(8,128)(2,1)} %get-tuple-element.256, bf16[8,512,128]{2,1,0:T(8,128)(2,1)} %get-tuple-element.255, ...), kind=kOutput, calls=%fused_computation.5.clone.1 | convolution fusion | flops 1098907136 | bytes 19044356 | tf_op jit(solution)/shard_map/cond/branch_1_fun/while/body/eval_jaxpr/dot_general | solution.py:78
  102.2 5.7 %copy-done = f32[512,8192]{1,0:T(8,128)} copy-done((f32[512,8192]{1,0:T(8,128)}, f32[512,8192]{1,0:T(8,128)S(1)}, u32[]{:S(2)}) %copy-start) | copy-done | bytes 16777240 | tf_op jit(solution)/shard_map/cond/branch_1_fun/while
  107.9 6.2 %fusion.38 = f32[512]{0:T(512)S(1)} fusion(f32[512,8192]{1,0:T(8,128)S(1)} %get-tuple-element.222, s32[512]{0:T(512)S(1)} %get-tuple-element.260, s32[8192]{0:T(1024)S(1)} %get-tuple-element.258, f32[512]{0:T(512)S(1)} %broadcast_maximum_fusion.2, s32[512]{0:T(512)S(1)} %get-tuple-element.259), kind=kLoop, calls=%fused_computation.7.clone.1 | loop fusion | flops 33553920 | bytes 16818176 | tf_op jit(solution)/shard_map/cond/branch_1_fun/while/body/eval_jaxpr/reduce_sum | solution.py:83
  114.0 1.3 dynamic_update_slice.14
  115.4 9.1 %fusion.39 = f32[1,512,128]{2,1,0:T(8,128)S(1)} fusion(bf16[8192,1,128]{2,0,1:T(8,128)(2,1)S(1)} %get-tuple-element.257, f32[512,8192]{1,0:T(8,128)} %copy-done, s32[512]{0:T(512)S(1)} %get-tuple-element.260, s32[8192]{0:T(1024)S(1)} %get-tuple-element.258, f32[512]{0:T(512)S(1)} %broadcast_maximum_fusion.2, s32[512]{0:T(512)S(1)} %get-tuple-element.259, ...), kind=kOutput, calls=%fused_computation.13.clone.1 | convolution fusion | flops 1107361792 | bytes 19177472 | tf_op jit(solution)/shard_map/cond/branch_1_fun/while/body/eval_jaxpr/dot_general | solution.py:84
  128.0 6.8 %fusion.37 = (f32[512]{0:T(512)S(1)}, f32[512,8192]{1,0:T(8,128)S(1)}) fusion(s32[512]{0:T(512)S(1)} %get-tuple-element.260, s32[8192]{0:T(1024)S(1)} %get-tuple-element.258, s32[512]{0:T(512)S(1)} %get-tuple-element.259, bf16[8192,1,128]{2,0,1:T(8,128)(2,1)} %get-tuple-element.256, bf16[8,512,128]{2,1,0:T(8,128)(2,1)} %get-tuple-element.255, ...), kind=kOutput, calls=%fused_computation.5.clone.1 | convolution fusion | flops 1098907136 | bytes 19044356 | tf_op jit(solution)/shard_map/cond/branch_1_fun/while/body/eval_jaxpr/dot_general | solution.py:78
  134.8 5.7 %copy-done = f32[512,8192]{1,0:T(8,128)} copy-done((f32[512,8192]{1,0:T(8,128)}, f32[512,8192]{1,0:T(8,128)S(1)}, u32[]{:S(2)}) %copy-start) | copy-done | bytes 16777240 | tf_op jit(solution)/shard_map/cond/branch_1_fun/while
  140.5 6.2 %fusion.38 = f32[512]{0:T(512)S(1)} fusion(f32[512,8192]{1,0:T(8,128)S(1)} %get-tuple-element.222, s32[512]{0:T(512)S(1)} %get-tuple-element.260, s32[8192]{0:T(1024)S(1)} %get-tuple-element.258, f32[512]{0:T(512)S(1)} %broadcast_maximum_fusion.2, s32[512]{0:T(512)S(1)} %get-tuple-element.259), kind=kLoop, calls=%fused_computation.7.clone.1 | loop fusion | flops 33553920 | bytes 16818176 | tf_op jit(solution)/shard_map/cond/branch_1_fun/while/body/eval_jaxpr/reduce_sum | solution.py:83
  146.7 1.3 dynamic_update_slice.14
  148.0 9.1 %fusion.39 = f32[1,512,128]{2,1,0:T(8,128)S(1)} fusion(bf16[8192,1,128]{2,0,1:T(8,128)(2,1)S(1)} %get-tuple-element.257, f32[512,8192]{1,0:T(8,128)} %copy-done, s32[512]{0:T(512)S(1)} %get-tuple-element.260, s32[8192]{0:T(1024)S(1)} %get-tuple-element.258, f32[512]{0:T(512)S(1)} %broadcast_maximum_fusion.2, s32[512]{0:T(512)S(1)} %get-tuple-element.259, ...), kind=kOutput, calls=%fused_computation.13.clone.1 | convolution fusion | flops 1107361792 | bytes 19177472 | tf_op jit(solution)/shard_map/cond/branch_1_fun/while/body/eval_jaxpr/dot_general | solution.py:84
  160.7 6.8 %fusion.37 = (f32[512]{0:T(512)S(1)}, f32[512,8192]{1,0:T(8,128)S(1)}) fusion(s32[512]{0:T(512)S(1)} %get-tuple-element.260, s32[8192]{0:T(1024)S(1)} %get-tuple-element.258, s32[512]{0:T(512)S(1)} %get-tuple-element.259, bf16[8192,1,128]{2,0,1:T(8,128)(2,1)} %get-tuple-element.256, bf16[8,512,128]{2,1,0:T(8,128)(2,1)} %get-tuple-element.255, ...), kind=kOutput, calls=%fused_computation.5.clone.1 | convolution fusion | flops 1098907136 | bytes 19044356 | tf_op jit(solution)/shard_map/cond/branch_1_fun/while/body/eval_jaxpr/dot_general | solution.py:78
  167.5 5.7 %copy-done = f32[512,8192]{1,0:T(8,128)} copy-done((f32[512,8192]{1,0:T(8,128)}, f32[512,8192]{1,0:T(8,128)S(1)}, u32[]{:S(2)}) %copy-start) | copy-done | bytes 16777240 | tf_op jit(solution)/shard_map/cond/branch_1_fun/while
  173.2 6.2 %fusion.38 = f32[512]{0:T(512)S(1)} fusion(f32[512,8192]{1,0:T(8,128)S(1)} %get-tuple-element.222, s32[512]{0:T(512)S(1)} %get-tuple-element.260, s32[8192]{0:T(1024)S(1)} %get-tuple-element.258, f32[512]{0:T(512)S(1)} %broadcast_maximum_fusion.2, s32[512]{0:T(512)S(1)} %get-tuple-element.259), kind=kLoop, calls=%fused_computation.7.clone.1 | loop fusion | flops 33553920 | bytes 16818176 | tf_op jit(solution)/shard_map/cond/branch_1_fun/while/body/eval_jaxpr/reduce_sum | solution.py:83
  179.4 1.3 dynamic_update_slice.14
  180.7 9.1 %fusion.39 = f32[1,512,128]{2,1,0:T(8,128)S(1)} fusion(bf16[8192,1,128]{2,0,1:T(8,128)(2,1)S(1)} %get-tuple-element.257, f32[512,8192]{1,0:T(8,128)} %copy-done, s32[512]{0:T(512)S(1)} %get-tuple-element.260, s32[8192]{0:T(1024)S(1)} %get-tuple-element.258, f32[512]{0:T(512)S(1)} %broadcast_maximum_fusion.2, s32[512]{0:T(512)S(1)} %get-tuple-element.259, ...), kind=kOutput, calls=%fused_computation.13.clone.1 | convolution fusion | flops 1107361792 | bytes 19177472 | tf_op jit(solution)/shard_map/cond/branch_1_fun/while/body/eval_jaxpr/dot_general | solution.py:84
  193.4 6.8 %fusion.37 = (f32[512]{0:T(512)S(1)}, f32[512,8192]{1,0:T(8,128)S(1)}) fusion(s32[512]{0:T(512)S(1)} %get-tuple-element.260, s32[8192]{0:T(1024)S(1)} %get-tuple-element.258, s32[512]{0:T(512)S(1)} %get-tuple-element.259, bf16[8192,1,128]{2,0,1:T(8,128)(2,1)} %get-tuple-element.256, bf16[8,512,128]{2,1,0:T(8,128)(2,1)} %get-tuple-element.255, ...), kind=kOutput, calls=%fused_computation.5.clone.1 | convolution fusion | flops 1098907136 | bytes 19044356 | tf_op jit(solution)/shard_map/cond/branch_1_fun/while/body/eval_jaxpr/dot_general | solution.py:78
  200.2 5.7 %copy-done = f32[512,8192]{1,0:T(8,128)} copy-done((f32[512,8192]{1,0:T(8,128)}, f32[512,8192]{1,0:T(8,128)S(1)}, u32[]{:S(2)}) %copy-start) | copy-done | bytes 16777240 | tf_op jit(solution)/shard_map/cond/branch_1_fun/while
  205.9 6.2 %fusion.38 = f32[512]{0:T(512)S(1)} fusion(f32[512,8192]{1,0:T(8,128)S(1)} %get-tuple-element.222, s32[512]{0:T(512)S(1)} %get-tuple-element.260, s32[8192]{0:T(1024)S(1)} %get-tuple-element.258, f32[512]{0:T(512)S(1)} %broadcast_maximum_fusion.2, s32[512]{0:T(512)S(1)} %get-tuple-element.259), kind=kLoop, calls=%fused_computation.7.clone.1 | loop fusion | flops 33553920 | bytes 16818176 | tf_op jit(solution)/shard_map/cond/branch_1_fun/while/body/eval_jaxpr/reduce_sum | solution.py:83
  212.0 1.3 dynamic_update_slice.14
  213.4 9.1 %fusion.39 = f32[1,512,128]{2,1,0:T(8,128)S(1)} fusion(bf16[8192,1,128]{2,0,1:T(8,128)(2,1)S(1)} %get-tuple-element.257, f32[512,8192]{1,0:T(8,128)} %copy-done, s32[512]{0:T(512)S(1)} %get-tuple-element.260, s32[8192]{0:T(1024)S(1)} %get-tuple-element.258, f32[512]{0:T(512)S(1)} %broadcast_maximum_fusion.2, s32[512]{0:T(512)S(1)} %get-tuple-element.259, ...), kind=kOutput, calls=%fused_computation.13.clone.1 | convolution fusion | flops 1107361792 | bytes 19177472 | tf_op jit(solution)/shard_map/cond/branch_1_fun/while/body/eval_jaxpr/dot_general | solution.py:84
  226.1 6.8 %fusion.37 = (f32[512]{0:T(512)S(1)}, f32[512,8192]{1,0:T(8,128)S(1)}) fusion(s32[512]{0:T(512)S(1)} %get-tuple-element.260, s32[8192]{0:T(1024)S(1)} %get-tuple-element.258, s32[512]{0:T(512)S(1)} %get-tuple-element.259, bf16[8192,1,128]{2,0,1:T(8,128)(2,1)} %get-tuple-element.256, bf16[8,512,128]{2,1,0:T(8,128)(2,1)} %get-tuple-element.255, ...), kind=kOutput, calls=%fused_computation.5.clone.1 | convolution fusion | flops 1098907136 | bytes 19044356 | tf_op jit(solution)/shard_map/cond/branch_1_fun/while/body/eval_jaxpr/dot_general | solution.py:78
  232.9 5.7 %copy-done = f32[512,8192]{1,0:T(8,128)} copy-done((f32[512,8192]{1,0:T(8,128)}, f32[512,8192]{1,0:T(8,128)S(1)}, u32[]{:S(2)}) %copy-start) | copy-done | bytes 16777240 | tf_op jit(solution)/shard_map/cond/branch_1_fun/while
  238.6 6.2 %fusion.38 = f32[512]{0:T(512)S(1)} fusion(f32[512,8192]{1,0:T(8,128)S(1)} %get-tuple-element.222, s32[512]{0:T(512)S(1)} %get-tuple-element.260, s32[8192]{0:T(1024)S(1)} %get-tuple-element.258, f32[512]{0:T(512)S(1)} %broadcast_maximum_fusion.2, s32[512]{0:T(512)S(1)} %get-tuple-element.259), kind=kLoop, calls=%fused_computation.7.clone.1 | loop fusion | flops 33553920 | bytes 16818176 | tf_op jit(solution)/shard_map/cond/branch_1_fun/while/body/eval_jaxpr/reduce_sum | solution.py:83
  244.7 1.3 dynamic_update_slice.14
  246.1 9.1 %fusion.39 = f32[1,512,128]{2,1,0:T(8,128)S(1)} fusion(bf16[8192,1,128]{2,0,1:T(8,128)(2,1)S(1)} %get-tuple-element.257, f32[512,8192]{1,0:T(8,128)} %copy-done, s32[512]{0:T(512)S(1)} %get-tuple-element.260, s32[8192]{0:T(1024)S(1)} %get-tuple-element.258, f32[512]{0:T(512)S(1)} %broadcast_maximum_fusion.2, s32[512]{0:T(512)S(1)} %get-tuple-element.259, ...), kind=kOutput, calls=%fused_computation.13.clone.1 | convolution fusion | flops 1107361792 | bytes 19177472 | tf_op jit(solution)/shard_map/cond/branch_1_fun/while/body/eval_jaxpr/dot_general | solution.py:84
  258.7 6.8 %fusion.37 = (f32[512]{0:T(512)S(1)}, f32[512,8192]{1,0:T(8,128)S(1)}) fusion(s32[512]{0:T(512)S(1)} %get-tuple-element.260, s32[8192]{0:T(1024)S(1)} %get-tuple-element.258, s32[512]{0:T(512)S(1)} %get-tuple-element.259, bf16[8192,1,128]{2,0,1:T(8,128)(2,1)} %get-tuple-element.256, bf16[8,512,128]{2,1,0:T(8,128)(2,1)} %get-tuple-element.255, ...), kind=kOutput, calls=%fused_computation.5.clone.1 | convolution fusion | flops 1098907136 | bytes 19044356 | tf_op jit(solution)/shard_map/cond/branch_1_fun/while/body/eval_jaxpr/dot_general | solution.py:78
  265.5 5.7 %copy-done = f32[512,8192]{1,0:T(8,128)} copy-done((f32[512,8192]{1,0:T(8,128)}, f32[512,8192]{1,0:T(8,128)S(1)}, u32[]{:S(2)}) %copy-start) | copy-done | bytes 16777240 | tf_op jit(solution)/shard_map/cond/branch_1_fun/while
  271.2 6.2 %fusion.38 = f32[512]{0:T(512)S(1)} fusion(f32[512,8192]{1,0:T(8,128)S(1)} %get-tuple-element.222, s32[512]{0:T(512)S(1)} %get-tuple-element.260, s32[8192]{0:T(1024)S(1)} %get-tuple-element.258, f32[512]{0:T(512)S(1)} %broadcast_maximum_fusion.2, s32[512]{0:T(512)S(1)} %get-tuple-element.259), kind=kLoop, calls=%fused_computation.7.clone.1 | loop fusion | flops 33553920 | bytes 16818176 | tf_op jit(solution)/shard_map/cond/branch_1_fun/while/body/eval_jaxpr/reduce_sum | solution.py:83
  277.4 1.3 dynamic_update_slice.14
  278.7 9.1 %fusion.39 = f32[1,512,128]{2,1,0:T(8,128)S(1)} fusion(bf16[8192,1,128]{2,0,1:T(8,128)(2,1)S(1)} %get-tuple-element.257, f32[512,8192]{1,0:T(8,128)} %copy-done, s32[512]{0:T(512)S(1)} %get-tuple-element.260, s32[8192]{0:T(1024)S(1)} %get-tuple-element.258, f32[512]{0:T(512)S(1)} %broadcast_maximum_fusion.2, s32[512]{0:T(512)S(1)} %get-tuple-element.259, ...), kind=kOutput, calls=%fused_computation.13.clone.1 | convolution fusion | flops 1107361792 | bytes 19177472 | tf_op jit(solution)/shard_map/cond/branch_1_fun/while/body/eval_jaxpr/dot_general | solution.py:84
  291.4 6.8 %fusion.37 = (f32[512]{0:T(512)S(1)}, f32[512,8192]{1,0:T(8,128)S(1)}) fusion(s32[512]{0:T(512)S(1)} %get-tuple-element.260, s32[8192]{0:T(1024)S(1)} %get-tuple-element.258, s32[512]{0:T(512)S(1)} %get-tuple-element.259, bf16[8192,1,128]{2,0,1:T(8,128)(2,1)} %get-tuple-element.256, bf16[8,512,128]{2,1,0:T(8,128)(2,1)} %get-tuple-element.255, ...), kind=kOutput, calls=%fused_computation.5.clone.1 | convolution fusion | flops 1098907136 | bytes 19044356 | tf_op jit(solution)/shard_map/cond/branch_1_fun/while/body/eval_jaxpr/dot_general | solution.py:78
  298.2 5.7 %copy-done = f32[512,8192]{1,0:T(8,128)} copy-done((f32[512,8192]{1,0:T(8,128)}, f32[512,8192]{1,0:T(8,128)S(1)}, u32[]{:S(2)}) %copy-start) | copy-done | bytes 16777240 | tf_op jit(solution)/shard_map/cond/branch_1_fun/while
  303.9 6.2 %fusion.38 = f32[512]{0:T(512)S(1)} fusion(f32[512,8192]{1,0:T(8,128)S(1)} %get-tuple-element.222, s32[512]{0:T(512)S(1)} %get-tuple-element.260, s32[8192]{0:T(1024)S(1)} %get-tuple-element.258, f32[512]{0:T(512)S(1)} %broadcast_maximum_fusion.2, s32[512]{0:T(512)S(1)} %get-tuple-element.259), kind=kLoop, calls=%fused_computation.7.clone.1 | loop fusion | flops 33553920 | bytes 16818176 | tf_op jit(solution)/shard_map/cond/branch_1_fun/while/body/eval_jaxpr/reduce_sum | solution.py:83
  310.1 1.3 dynamic_update_slice.14
  311.4 9.1 %fusion.39 = f32[1,512,128]{2,1,0:T(8,128)S(1)} fusion(bf16[8192,1,128]{2,0,1:T(8,128)(2,1)S(1)} %get-tuple-element.257, f32[512,8192]{1,0:T(8,128)} %copy-done, s32[512]{0:T(512)S(1)} %get-tuple-element.260, s32[8192]{0:T(1024)S(1)} %get-tuple-element.258, f32[512]{0:T(512)S(1)} %broadcast_maximum_fusion.2, s32[512]{0:T(512)S(1)} %get-tuple-element.259, ...), kind=kOutput, calls=%fused_computation.13.clone.1 | convolution fusion | flops 1107361792 | bytes 19177472 | tf_op jit(solution)/shard_map/cond/branch_1_fun/while/body/eval_jaxpr/dot_general | solution.py:84
  324.1 6.8 %fusion.37 = (f32[512]{0:T(512)S(1)}, f32[512,8192]{1,0:T(8,128)S(1)}) fusion(s32[512]{0:T(512)S(1)} %get-tuple-element.260, s32[8192]{0:T(1024)S(1)} %get-tuple-element.258, s32[512]{0:T(512)S(1)} %get-tuple-element.259, bf16[8192,1,128]{2,0,1:T(8,128)(2,1)} %get-tuple-element.256, bf16[8,512,128]{2,1,0:T(8,128)(2,1)} %get-tuple-element.255, ...), kind=kOutput, calls=%fused_computation.5.clone.1 | convolution fusion | flops 1098907136 | bytes 19044356 | tf_op jit(solution)/shard_map/cond/branch_1_fun/while/body/eval_jaxpr/dot_general | solution.py:78
  330.9 5.7 %copy-done = f32[512,8192]{1,0:T(8,128)} copy-done((f32[512,8192]{1,0:T(8,128)}, f32[512,8192]{1,0:T(8,128)S(1)}, u32[]{:S(2)}) %copy-start) | copy-done | bytes 16777240 | tf_op jit(solution)/shard_map/cond/branch_1_fun/while
  336.6 6.2 %fusion.38 = f32[512]{0:T(512)S(1)} fusion(f32[512,8192]{1,0:T(8,128)S(1)} %get-tuple-element.222, s32[512]{0:T(512)S(1)} %get-tuple-element.260, s32[8192]{0:T(1024)S(1)} %get-tuple-element.258, f32[512]{0:T(512)S(1)} %broadcast_maximum_fusion.2, s32[512]{0:T(512)S(1)} %get-tuple-element.259), kind=kLoop, calls=%fused_computation.7.clone.1 | loop fusion | flops 33553920 | bytes 16818176 | tf_op jit(solution)/shard_map/cond/branch_1_fun/while/body/eval_jaxpr/reduce_sum | solution.py:83
  342.7 1.3 dynamic_update_slice.14
  344.1 9.1 %fusion.39 = f32[1,512,128]{2,1,0:T(8,128)S(1)} fusion(bf16[8192,1,128]{2,0,1:T(8,128)(2,1)S(1)} %get-tuple-element.257, f32[512,8192]{1,0:T(8,128)} %copy-done, s32[512]{0:T(512)S(1)} %get-tuple-element.260, s32[8192]{0:T(1024)S(1)} %get-tuple-element.258, f32[512]{0:T(512)S(1)} %broadcast_maximum_fusion.2, s32[512]{0:T(512)S(1)} %get-tuple-element.259, ...), kind=kOutput, calls=%fused_computation.13.clone.1 | convolution fusion | flops 1107361792 | bytes 19177472 | tf_op jit(solution)/shard_map/cond/branch_1_fun/while/body/eval_jaxpr/dot_general | solution.py:84
  354.0 1.9 divide_convert_fusion
  355.9 2.0 copy.41
  358.4 6.8 %reduce.2 = bf16[512,1024]{1,0:T(8,128)(2,1)S(1)} reduce(bf16[512,1,1024]{2,1,0:T(2,128)(2,1)S(1)} %bitcast.79, bf16[]{:T(256)} %broadcast.102), dimensions={1}, to_apply=%bitcast.60.reduce_sub_computation | reduce | bytes 2097154
  366.0 34.3 %all_to_all.39 = bf16[8,2,32768]{2,1,0:T(2,128)(2,1)S(1)} all-to-all(bf16[8,2,32768]{2,1,0:T(2,128)(2,1)S(1)} %reshape.79), channel_id=1, replica_groups=mesh['parts'=2,'uly'=8,'blk'=16] {'uly'}, dimensions={0} | all-to-all | bytes 2097152 | tf_op jit(solution)/shard_map/all_to_all | solution.py:96
  400.3 1.0 reshape.80
  401.7 1.1 copy.48
  (73 shorter events, 19.2 us)
Async XLA Ops:
  6.5 80.9 %all-gather.2.cloned.1.call-start = ((), (), s32[]{:S(2)}) async-start(), calls=%async_computation.3 | async-start | bytes 4456448 | tf_op jit(solution)/shard_map/all_gather | solution.py:64
  40.6 20.1 %all-to-all-start.1 = ((bf16[8,1,64,1024]{3,2,1,0:T(8,128)(2,1)}), bf16[8,1,64,1024]{3,2,1,0:T(8,128)(2,1)S(1)}, u32[]{:S(2)}, u32[]{:S(2)}) async-start(bf16[8,1,64,1024]{3,2,1,0:T(8,128)(2,1)} %bitcast_dynamic-update-slice_fusion), calls=%async_computation.1 | async-start | bytes 2097152 | tf_op jit(solution)/shard_map/all_to_all | solution.py:14
  102.2 5.7 %copy-start = (f32[512,8192]{1,0:T(8,128)}, f32[512,8192]{1,0:T(8,128)S(1)}, u32[]{:S(2)}) copy-start(f32[512,8192]{1,0:T(8,128)S(1)} %get-tuple-element.222) | copy-start | bytes 50331652 | tf_op jit(solution)/shard_map/cond/branch_1_fun/while
  134.8 5.7 %copy-start = (f32[512,8192]{1,0:T(8,128)}, f32[512,8192]{1,0:T(8,128)S(1)}, u32[]{:S(2)}) copy-start(f32[512,8192]{1,0:T(8,128)S(1)} %get-tuple-element.222) | copy-start | bytes 50331652 | tf_op jit(solution)/shard_map/cond/branch_1_fun/while
  167.5 5.7 %copy-start = (f32[512,8192]{1,0:T(8,128)}, f32[512,8192]{1,0:T(8,128)S(1)}, u32[]{:S(2)}) copy-start(f32[512,8192]{1,0:T(8,128)S(1)} %get-tuple-element.222) | copy-start | bytes 50331652 | tf_op jit(solution)/shard_map/cond/branch_1_fun/while
  200.2 5.7 %copy-start = (f32[512,8192]{1,0:T(8,128)}, f32[512,8192]{1,0:T(8,128)S(1)}, u32[]{:S(2)}) copy-start(f32[512,8192]{1,0:T(8,128)S(1)} %get-tuple-element.222) | copy-start | bytes 50331652 | tf_op jit(solution)/shard_map/cond/branch_1_fun/while
  232.8 5.7 %copy-start = (f32[512,8192]{1,0:T(8,128)}, f32[512,8192]{1,0:T(8,128)S(1)}, u32[]{:S(2)}) copy-start(f32[512,8192]{1,0:T(8,128)S(1)} %get-tuple-element.222) | copy-start | bytes 50331652 | tf_op jit(solution)/shard_map/cond/branch_1_fun/while
  265.5 5.7 %copy-start = (f32[512,8192]{1,0:T(8,128)}, f32[512,8192]{1,0:T(8,128)S(1)}, u32[]{:S(2)}) copy-start(f32[512,8192]{1,0:T(8,128)S(1)} %get-tuple-element.222) | copy-start | bytes 50331652 | tf_op jit(solution)/shard_map/cond/branch_1_fun/while
  298.2 5.7 %copy-start = (f32[512,8192]{1,0:T(8,128)}, f32[512,8192]{1,0:T(8,128)S(1)}, u32[]{:S(2)}) copy-start(f32[512,8192]{1,0:T(8,128)S(1)} %get-tuple-element.222) | copy-start | bytes 50331652 | tf_op jit(solution)/shard_map/cond/branch_1_fun/while
  330.8 5.7 %copy-start = (f32[512,8192]{1,0:T(8,128)}, f32[512,8192]{1,0:T(8,128)S(1)}, u32[]{:S(2)}) copy-start(f32[512,8192]{1,0:T(8,128)S(1)} %get-tuple-element.222) | copy-start | bytes 50331652 | tf_op jit(solution)/shard_map/cond/branch_1_fun/while
Sparse Core Ops, SparseCore 0:
  28.2 59.1 all-gather.1
